TPU v7x, 512 devices: a whole 4x4x16 slice. The times are simulated.
512 devices in a mesh: freq: 16 (over x, z_lo), line: 32 (over z_hi, y, core).
Axes of the slice: x: 4, y: 4, z: 16 (z_hi: 4, z_lo: 4; z = z_hi * 4 + z_lo), core: 2. Of those that a mesh axis runs over, the one named last changes fastest.
Arguments:
- field: float32 [16, 2, 4, 96, 64, 256], P('freq', None, None, None, 'line'), may hold values from -6 to 6
- live_count: int32 [64], P('line'), may hold values from 64 to 256
- line_owner: int32 [64], replicated, may hold values from 0 to 63, each once
- decomposer: float32 [16, 2, 4, 4, 64, 256], P('freq', None, None, None, 'line'), may hold values from -1.4 to 2.4
- reflection: bfloat16 [16, 1024, 2, 16384], P('freq', None, None, 'line'), may hold values from -0.0625 to 0.0625
- direct_wave: float32 [1024, 16, 2, 384], P('line', 'freq'), may hold values from -6 to 6
Outputs:
- focusing: float32 [1024, 16, 2, 384], P('line', 'freq')
- trace_energy: float32 [1024], P('line')
Inputs may be any that keep to these rules, and one draw needn't show every extreme that they name: `line_owner`: each crossline position appears once.
All inputs are finite; a program needn't handle non-finite values.
Results may differ from a plain program's by a relative error of at most 0.0023.
Values may be sent and summed in bfloat16 or wider, within the bound.
No kernel may reach another device: no remote copies, remote signals or barrier semaphores. Data moves between devices by JAX's collectives and lax.ppermute only.
A program may use at most 64 MiB of HBM per device.

v0:
```python
import math
import jax
import jax.numpy as jnp
from jax import lax
from jax.sharding import Mesh
from jax.sharding import PartitionSpec as P

LINE = ("line_0", "line_1", "line_2")


def in_blocks(shard, dim, count):
    before, after = (shard.shape[:dim], shard.shape[dim + 1 :])
    return jnp.moveaxis(shard.reshape(*before, count, -1, *after), dim, 0)


def scatter_pairs(shard, chips, core, dim):
    sizes = (lax.axis_size(chips), lax.axis_size(core))
    blocks = in_blocks(shard, dim, sizes[0] * sizes[1])
    inside = blocks.shape[1:]
    blocks = blocks.reshape(*sizes, *inside).swapaxes(0, 1).reshape(-1, *inside)
    blocks = lax.psum_scatter(blocks, core, scatter_dimension=0, tiled=True)
    return lax.psum_scatter(blocks, chips, scatter_dimension=0, tiled=True)[0]


def sent_to_all(shard, axis):
    count = lax.axis_size(axis)
    return lax.all_to_all(
        jnp.broadcast_to(shard[None], (count, *shard.shape)), axis, 0, 0, tiled=True
    )


def over_copies(shard, axis):
    return sent_to_all(shard, axis).sum(axis=0)


def phase_tables(line_owner, length):
    wavenum = jnp.arange(length, dtype=jnp.int32)
    products = wavenum[:, None] * line_owner[None, :] % length
    angles = products.astype(jnp.float32) * (2.0 * math.pi / length)
    return (jnp.cos(angles), jnp.sin(angles))


def decompose(operator, spectrum):
    real_rows = []
    imag_rows = []
    for target in range(4):
        real_sum = None
        imag_sum = None
        for source in range(4):
            weight_real = operator[:, 0, target, source][:, None]
            weight_imag = operator[:, 1, target, source][:, None]
            field_real = spectrum[:, 0, source]
            field_imag = spectrum[:, 1, source]
            term_real = weight_real * field_real - weight_imag * field_imag
            term_imag = weight_real * field_imag + weight_imag * field_real
            real_sum = term_real if real_sum is None else real_sum + term_real
            imag_sum = term_imag if imag_sum is None else imag_sum + term_imag
        real_rows.append(real_sum)
        imag_rows.append(imag_sum)
    return jnp.stack([jnp.stack(real_rows, 1), jnp.stack(imag_rows, 1)], 1)


def on_device(field, live_count, line_owner, decomposer, reflection, direct_wave):
    length = line_owner.shape[0]
    receivers = field.shape[5]
    cosine, sine_table = phase_tables(line_owner, length)
    forward_table = jnp.stack([jnp.stack([cosine, sine_table]), jnp.stack([-sine_table, cosine])])
    inverse_table = (
        jnp.stack([jnp.stack([cosine.T, -sine_table.T]), jnp.stack([sine_table.T, cosine.T])])
        / length
    )
    live_mask = jnp.arange(receivers, dtype=jnp.int32)[None, :] < live_count[:, None]
    live_field = jnp.where(live_mask, field, jnp.float32(0.0))
    operator = lax.all_gather(decomposer, LINE, axis=4, tiled=True)
    every_line = lax.all_to_all(live_field, LINE, split_axis=3, concat_axis=4, tiled=True)
    space_all = jnp.einsum(
        "yxjk,fxiokr->fyiojr",
        inverse_table,
        decompose(
            operator,
            jnp.einsum(
                "yxkj,fxiojr->fyiokr", forward_table, every_line, precision=lax.Precision.HIGHEST
            ),
        ),
        precision=lax.Precision.HIGHEST,
    )
    wavefield = lax.all_to_all(
        space_all.astype(jnp.bfloat16), LINE, split_axis=4, concat_axis=3, tiled=True
    )
    freq_count = wavefield.shape[0]
    channels = wavefield.shape[2] * wavefield.shape[3]
    positions = wavefield.shape[4] * wavefield.shape[5]
    wave_bf = wavefield.reshape(freq_count, 2, channels, positions)
    real_part = wave_bf[:, 0]
    imag_part = wave_bf[:, 1]
    stacked = jnp.stack(
        [jnp.stack([real_part, imag_part], 1), jnp.stack([-imag_part, real_part], 1)], 1
    )
    reflected = scatter_pairs(
        jnp.einsum("fsxq,fxocq->sfoc", reflection, stacked, preferred_element_type=jnp.float32),
        ("line_0", "line_1"),
        "line_2",
        0,
    )
    focusing = direct_wave - reflected
    total_freqs = freq_count * lax.axis_size("freq")
    freq_index = lax.axis_index("freq") * freq_count + jnp.arange(freq_count, dtype=jnp.int32)
    weights = 2.0 * (freq_index + 1).astype(jnp.float32) / (total_freqs * (total_freqs + 1))
    partial_value = jnp.sum(jnp.sum(reflected * reflected, axis=(2, 3)) * weights[None, :], axis=1)
    energy_sum = over_copies(partial_value, "freq")
    trace_energy = jnp.sqrt(energy_sum / (2 * channels) + 1e-06)
    return (focusing, trace_energy)


def solution(mesh):
    finer = Mesh(
        mesh.devices.reshape(mesh.shape["freq"], 4, 4, 2), ("freq", "line_0", "line_1", "line_2")
    )
    in_specs = (
        P("freq", None, None, None, LINE, None),
        P(LINE),
        P(),
        P("freq", None, None, None, LINE, None),
        P("freq", None, None, LINE),
        P(LINE, "freq", None, None),
    )
    out_specs = (P(LINE, "freq", None, None), P(LINE))
    return jax.shard_map(
        on_device, mesh=finer, in_specs=in_specs, out_specs=out_specs, check_vma=False
    )
```

profile of v0, /device:TPU:8, one launch (start us, length us, event | category | flops | bytes accessed | tf_op | source)
XLA Modules:
  0.0 385.9 jit_solution(8191804675190697036)
XLA Ops:
  7.2 1.5 copy.86
  8.7 0.7 iota_compare_fusion
  9.4 3.5 copy_select_fusion
  12.9 18.5 %all-to-all-start = ((f32[1,2,4,96,2,256]{5,4,2,1,0,3:T(2,128)}), f32[1,2,4,96,2,256]{5,4,2,1,0,3:T(2,128)S(1)}, u32[]{:S(2)}, u32[]{:S(2)}) async-start(f32[1,2,4,96,2,256]{5,4,2,1,0,3:T(2,128)} %copy_select_fusion), calls=%async_computation | async-start | bytes 3145728 | tf_op jit(solution)/shard_map/all_to_all | solution.py:75
  31.7 0.7 maximum_bitcast_fusion.8
  33.0 100.7 %all-gather.2.cloned.1.call-done = f32[1,2,4,4,64,256]{5,3,2,1,0,4:T(4,128)} async-done(((f32[1,2,4,4,2,256]{5,3,2,1,0,4:T(4,128)}), f32[1,2,4,4,64,256]{5,3,2,1,0,4:T(4,128)}) %all-gather.2.cloned.1.call-update) | async-done | bytes 2097168 | tf_op jit(solution)/shard_map/all_gather | solution.py:74
  133.7 3.3 fusion.51
  137.0 4.3 %fusion.50 = (f32[1,1,1,1,64,256]{5,3,2,1,0,4:T(1,128)S(1)}, f32[1,1,1,1,64,256]{5,3,2,1,0,4:T(1,128)S(1)}, f32[1,1,1,1,64,256]{5,3,2,1,0,4:T(1,128)S(1)}, f32[1...) fusion(f32[1,2,4,4,64,256]{5,3,2,1,0,4:T(4,128)} %all-gather.2., ...), kind=kLoop, calls=%fused_computation.116 | loop fusion | bytes 2490368 | tf_op jit(solution)/shard_map/slice | solution.py:50
  141.4 0.7 copy_bitcast_fusion.30
  142.1 0.7 copy_bitcast_fusion.18
  142.7 0.7 copy_bitcast_fusion.20
  144.7 0.7 copy_bitcast_fusion.10
  146.0 0.7 copy_bitcast_fusion.14
  147.3 0.7 copy_bitcast_fusion.2
  148.6 0.7 copy_bitcast_fusion.6
  149.9 0.9 copy.201
  150.8 1.1 reshape.1466
  151.9 2.5 fusion.12
  158.5 0.7 copy-done.26
  159.3 1.6 fusion.17
  160.8 0.8 copy.97
  161.6 49.5 %all_to_all.36 = bf16[1,2,4,3,64,256]{5,1,3,2,0,4:T(2,128)(2,1)S(1)} all-to-all(bf16[1,2,4,3,64,256]{5,1,3,2,0,4:T(2,128)(2,1)S(1)} %copy.97), channel_id=1, replica_groups=mesh['freq'=16,'line_0'=4,'line_1'=4,'line_2'=2] {'line_0','line_1','lin..., dimensions={4} | all-to-all | bytes 1572864 | tf_op jit(solution)/shard_map/all_to_all | solution.py:87
  212.9 1.4 copy-done.30
  214.4 3.5 fusion.3
  217.8 2.4 copy.100
  220.2 1.9 copy.101
  222.2 18.9 %reduce-scatter.3.cloned.1.call-done = f32[16,32,1,2,384]{4,1,3,2,0:T(8,128)} async-done(((f32[32,32,1,2,384]{4,1,3,2,0:T(8,128)}), f32[16,32,1,2,384]{4,1,3,2,0:T(8,128)}) %reduce-scatter.3.cloned.1.call-update) | async-done | bytes 1572880 | tf_op jit(solution)/shard_map/reduce_scatter | solution.py:21
  241.1 122.4 %reduce-scatter.5.cloned.1.call-done = f32[1,32,1,2,384]{4,1,3,2,0:T(8,128)} async-done(((f32[16,32,1,2,384]{4,1,3,2,0:T(8,128)}), f32[1,32,1,2,384]{4,1,3,2,0:T(8,128)}) %reduce-scatter.5.cloned.1.call-update) | async-done | bytes 98320 | tf_op jit(solution)/shard_map/reduce_scatter | solution.py:22
  363.5 1.0 fusion.26
  365.1 5.7 %all-to-all-start.2 = ((f32[16,1,32]{2,1,0:T(1,128)}), f32[16,1,32]{2,1,0:T(1,128)S(1)}, u32[]{:S(2)}, u32[]{:S(2)}) async-start(f32[16,1,32]{2,1,0:T(1,128)} %broadcast_in_dim.12), calls=%async_computation.4 | async-start | bytes 16384 | tf_op jit(solution)/shard_map/all_to_all | solution.py:27
  370.9 0.7 copy.104
  371.6 7.2 %all-to-all-done.2 = f32[16,1,32]{2,1,0:T(1,128)S(1)} async-done(((f32[16,1,32]{2,1,0:T(1,128)}), f32[16,1,32]{2,1,0:T(1,128)S(1)}, u32[]{:S(2)}, u32[]{:S(2)}) %all-to-all-start.2) | async-done | bytes 2080 | tf_op jit(solution)/shard_map/all_to_all | solution.py:27
  (97 shorter events, 11.8 us)
Async XLA Ops:
  7.2 126.5 %all-gather.2.cloned.1.call-start = ((), (), s32[]{:S(2)}) async-start(), calls=%async_computation.5 | async-start | bytes 2162688 | tf_op jit(solution)/shard_map/all_gather | solution.py:74
  12.9 18.5 %copy-start.29 = (s32[64]{0:T(128)S(1)}, s32[64]{0:T(128)}, u32[]{:S(2)}) copy-start(s32[64]{0:T(128)} %param.8) | copy-start | bytes 772
  12.9 137.0 %all-to-all-start = ((f32[1,2,4,96,2,256]{5,4,2,1,0,3:T(2,128)}), f32[1,2,4,96,2,256]{5,4,2,1,0,3:T(2,128)S(1)}, u32[]{:S(2)}, u32[]{:S(2)}) async-start(f32[1,2,4,96,2,256]{5,4,2,1,0,3:T(2,128)} %copy_select_fusion), calls=%async_computation | async-start | bytes 3145728 | tf_op jit(solution)/shard_map/all_to_all | solution.py:75
  31.4 209.7 %reduce-scatter.3.cloned.1.call-start = ((), (), s32[]{:S(2)}) async-start(), calls=%async_computation.6 | async-start | bytes 4718592 | tf_op jit(solution)/shard_map/reduce_scatter | solution.py:21
  151.9 2.5 copy-start.2
  151.9 2.5 copy-start.3
  154.6 0.9 copy-start.1
  154.6 0.9 copy-start.4
  154.6 0.9 copy-start.5
  154.6 0.9 copy-start.6
  154.6 1.0 copy-start.7
  154.6 1.0 copy-start.10
  154.6 1.0 copy-start.11
  155.8 0.9 copy-start.9
  155.8 0.9 copy-start.12
  155.8 0.9 copy-start.13
  155.8 0.9 copy-start.14
  155.8 1.0 copy-start.15
  155.8 1.0 copy-start.18
  155.9 1.0 copy-start.19
  157.0 0.9 copy-start.17
  157.0 0.9 copy-start.20
  157.0 0.9 copy-start.21
  157.0 0.9 copy-start.22
  157.1 1.0 copy-start.23
  157.1 1.0 copy-start.24
  157.1 1.0 copy-start.25
  158.4 0.9 copy-start.27
  212.8 1.6 copy-start.30
  222.1 141.4 %copy-start.28 = (f32[32,1,2,384]{3,2,1,0:T(2,128)S(1)}, f32[32,1,2,384]{3,2,1,0:T(2,128)}, u32[]{:S(2)}) copy-start(f32[32,1,2,384]{3,2,1,0:T(2,128)} %param.11) | copy-start | bytes 294916
  222.2 141.3 %reduce-scatter.5.cloned.1.call-start = ((), (), s32[]{:S(2)}) async-start(), calls=%async_computation.7 | async-start | bytes 1671168 | tf_op jit(solution)/shard_map/reduce_scatter | solution.py:22
  365.1 13.7 %all-to-all-start.2 = ((f32[16,1,32]{2,1,0:T(1,128)}), f32[16,1,32]{2,1,0:T(1,128)S(1)}, u32[]{:S(2)}, u32[]{:S(2)}) async-start(f32[16,1,32]{2,1,0:T(1,128)} %broadcast_in_dim.12), calls=%async_computation.4 | async-start | bytes 16384 | tf_op jit(solution)/shard_map/all_to_all | solution.py:27
  (4 other events, 3.4 us)
Sparse Core Ops, SparseCore 0:
  11.1 122.5 all-gather.1
  222.3 18.7 reduce-scatter.2
  245.2 118.2 reduce-scatter.4
where the time goes:
time: 387 us; the launch traced here: 386 us
  waiting for transfers between devices  249 us (64%)
  blocking collectives  49.5 us (13%)
  local copies, waits for them, and re-layouts  32.4 us (8%)
  starting transfers between devices  24.3 us (6%)
  between operations  14.2 us (4%)
  other arithmetic  8.75 us (2%)
  matrix products  7.49 us (2%)
    reduce_scatter x1, waiting for transfers between devices, scatter_pairs(): return lax.psum_scatter(blocks, chips, scatter_dimension=0, tiled=True)[0]  122 us
    all_gather x1, waiting for transfers between devices, on_device(): operator = lax.all_gather(decomposer, LINE, axis=4, tiled=True)  101 us
    all_to_all x1, blocking collectives, on_device(): lax.all_to_all(space_all.astype(jnp.bfloat16), LINE, split_axis=4, concat...  49.5 us
    reduce_scatter x1, waiting for transfers between devices, scatter_pairs(): blocks = lax.psum_scatter(blocks, core, scatter_dimension=0, tiled=True)  18.9 us
    all_to_all x1, starting transfers between devices, on_device(): lax.all_to_all(live_field, LINE, split_axis=3, concat_axis=4, tiled=True)  18.5 us
    unnamed x80, local copies, waits for them, and re-layouts  15.5 us
  transfers between devices with their start and end apart: 5, of which 4 were waited for; matrix products, arithmetic and copies ran while one was open for 6% of the time, Pallas kernels for 0%

commit v1 on v0

--- a/solution.py
+++ b/solution.py
@@ -4,6 +4,7 @@
 from jax import lax
 from jax.sharding import Mesh
 from jax.sharding import PartitionSpec as P
+from jax.lax import all_to_all, axis_size
 
 LINE = ("line_0", "line_1", "line_2")
 
@@ -61,6 +62,13 @@
 
 
 def on_device(field, live_count, line_owner, decomposer, reflection, direct_wave):
+
+    def pass_grid(message):
+        return jnp.concatenate(
+            all_to_all(jnp.stack([message] * axis_size(LINE)), LINE, split_axis=0, concat_axis=0),
+            axis=4,
+        )
+
     length = line_owner.shape[0]
     receivers = field.shape[5]
     cosine, sine_table = phase_tables(line_owner, length)
@@ -71,7 +79,7 @@
     )
     live_mask = jnp.arange(receivers, dtype=jnp.int32)[None, :] < live_count[:, None]
     live_field = jnp.where(live_mask, field, jnp.float32(0.0))
-    operator = lax.all_gather(decomposer, LINE, axis=4, tiled=True)
+    operator = pass_grid(decomposer)
     every_line = lax.all_to_all(live_field, LINE, split_axis=3, concat_axis=4, tiled=True)
     space_all = jnp.einsum(
         "yxjk,fxiokr->fyiojr",

time: 387 us -> 444 us (1.15)
  blocking collectives: 49.5 us -> 144 us
  local copies, waits for them, and re-layouts: 32.4 us -> 20.2 us
  starting transfers between devices: 24.3 us -> 12.4 us
  waiting for transfers between devices: 249 us -> 239 us
    all_gather x1 -> x0, waiting for transfers between devices: 101 us -> none  [on_device(): operator = lax.all_gather(decomposer, LINE, axis=4, tiled=True)]
    all_to_all x0 -> x1, blocking collectives: none -> 95.7 us  [on_device(): lax.all_to_all(live_field, LINE, split_axis=3, concat_axis=4, tiled=True)]
    all_to_all x1, waiting for transfers between devices: 0.01 us -> 92.7 us  [pass_grid(): all_to_all(jnp.stack([message] * axis_size(LINE)), LINE, split_axis=0, co...]
    unnamed x80 -> x25, local copies, waits for them, and re-layouts: 15.5 us -> 2.36 us
    all_to_all x1, starting transfers between devices: 18.5 us -> 6.47 us  [pass_grid(): all_to_all(jnp.stack([message] * axis_size(LINE)), LINE, split_axis=0, co...]
  transfers between devices with their start and end apart: 5 -> 4, of which waited for: 4 -> 4; matrix products, arithmetic and copies ran while one was open for 6% -> 2% of each run, Pallas kernels for 0% -> 0%
where the time goes in v1:
time: 444 us; the launch traced here: 443 us
  waiting for transfers between devices  239 us (54%)
  blocking collectives  144 us (32%)
  local copies, waits for them, and re-layouts  20.2 us (5%)
  between operations  14.4 us (3%)
  starting transfers between devices  12.4 us (3%)
  matrix products  6.58 us (1%)
  other arithmetic  6.33 us (1%)
    reduce_scatter x1, waiting for transfers between devices, scatter_pairs(): return lax.psum_scatter(blocks, chips, scatter_dimension=0, tiled=True)[0]  123 us
    all_to_all x1, blocking collectives, on_device(): lax.all_to_all(live_field, LINE, split_axis=3, concat_axis=4, tiled=True)  95.7 us
    all_to_all x1, waiting for transfers between devices, pass_grid(): all_to_all(jnp.stack([message] * axis_size(LINE)), LINE, split_axis=0, co...  92.7 us
    all_to_all x1, blocking collectives, on_device(): lax.all_to_all(space_all.astype(jnp.bfloat16), LINE, split_axis=4, concat...  48.8 us
    reduce_scatter x1, waiting for transfers between devices, scatter_pairs(): blocks = lax.psum_scatter(blocks, core, scatter_dimension=0, tiled=True)  16.1 us
  transfers between devices with their start and end apart: 4, of which 4 were waited for; matrix products, arithmetic and copies ran while one was open for 2% of the time, Pallas kernels for 0%

profile of v1, /device:TPU:8, one launch (start us, length us, event | category | flops | bytes accessed | tf_op | source)
XLA Modules:
  0.0 443.2 jit_solution(11182954298783934100)
XLA Ops:
  7.2 0.7 iota_compare_fusion
  7.9 2.3 copy_select_fusion
  10.2 95.7 %all_to_all.41 = f32[1,2,4,96,2,256]{5,4,2,1,0,3:T(2,128)S(1)} all-to-all(f32[1,2,4,96,2,256]{5,4,2,1,0,3:T(2,128)S(1)} %copy_select_fusion), channel_id=1, replica_groups=mesh['freq'=16,'line_0'=4,'line_1'=4,'line_2'=2] {'line_0','line_1','lin..., dimensions={3} | all-to-all | bytes 3145728 | tf_op jit(solution)/shard_map/all_to_all | solution.py:83
  105.9 2.3 stack.40
  108.2 6.5 %all-to-all-start = ((f32[32,1,2,4,4,2,256]{6,5,4,3,2,1,0:T(2,128)}), f32[32,1,2,4,4,2,256]{6,5,4,3,2,1,0:T(2,128)}, u32[]{:S(2)}, u32[]{:S(2)}) async-start(f32[32,1,2,4,4,2,256]{6,5,4,3,2,1,0:T(2,128)} %stack.40), calls=%async_computation | async-start | bytes 4194304 | tf_op jit(solution)/shard_map/all_to_all | solution.py:68
  114.7 0.2 reduce-scatter.3.cloned.1.call-start
  114.9 0.3 fusion.45
  115.3 2.0 copy.218
  117.3 2.4 reshape.1477
  119.7 1.6 fusion.12
  121.2 92.7 %all-to-all-done = f32[32,1,2,4,4,2,256]{6,5,4,3,2,1,0:T(2,128)} async-done(((f32[32,1,2,4,4,2,256]{6,5,4,3,2,1,0:T(2,128)}), f32[32,1,2,4,4,2,256]{6,5,4,3,2,1,0:T(2,128)}, u32[]{:S(2)}, u32[]{:S(2)}) %all-to-all-start) | async-done | bytes 2097184 | tf_op jit(solution)/shard_map/all_to_all | solution.py:68
  213.9 2.1 copy.103
  216.1 1.0 fusion.50
  217.1 0.7 fusion.51
  219.4 1.6 fusion.17
  221.0 0.8 copy.114
  221.8 48.8 %all_to_all.42 = bf16[1,2,4,3,64,256]{5,1,3,2,0,4:T(2,128)(2,1)S(1)} all-to-all(bf16[1,2,4,3,64,256]{5,1,3,2,0,4:T(2,128)(2,1)S(1)} %copy.114), channel_id=1, replica_groups=mesh['freq'=16,'line_0'=4,'line_1'=4,'line_2'=2] {'line_0','line_1','lin..., dimensions={4} | all-to-all | bytes 1572864 | tf_op jit(solution)/shard_map/all_to_all | solution.py:95
  270.6 0.6 copy.219
  271.3 0.5 reshape.1473
  271.8 0.5 stack.56
  272.4 1.4 copy-done.3
  273.9 3.5 fusion.3
  277.3 2.4 copy.117
  279.7 1.9 copy.118
  281.7 16.1 %reduce-scatter.3.cloned.1.call-done = f32[16,32,1,2,384]{4,1,3,2,0:T(8,128)} async-done(((f32[32,32,1,2,384]{4,1,3,2,0:T(8,128)}), f32[16,32,1,2,384]{4,1,3,2,0:T(8,128)}) %reduce-scatter.3.cloned.1.call-update) | async-done | bytes 1572880 | tf_op jit(solution)/shard_map/reduce_scatter | solution.py:22
  297.8 122.7 %reduce-scatter.5.cloned.1.call-done = f32[1,32,1,2,384]{4,1,3,2,0:T(8,128)} async-done(((f32[16,32,1,2,384]{4,1,3,2,0:T(8,128)}), f32[1,32,1,2,384]{4,1,3,2,0:T(8,128)}) %reduce-scatter.5.cloned.1.call-update) | async-done | bytes 98320 | tf_op jit(solution)/shard_map/reduce_scatter | solution.py:23
  420.6 1.0 fusion.26
  421.6 0.6 broadcast_in_dim.12
  422.2 5.7 %all-to-all-start.3 = ((f32[16,1,32]{2,1,0:T(1,128)}), f32[16,1,32]{2,1,0:T(1,128)S(1)}, u32[]{:S(2)}, u32[]{:S(2)}) async-start(f32[16,1,32]{2,1,0:T(1,128)} %broadcast_in_dim.12), calls=%async_computation.5 | async-start | bytes 16384 | tf_op jit(solution)/shard_map/all_to_all | solution.py:28
  427.9 0.7 copy.121
  428.6 7.2 %all-to-all-done.3 = f32[16,1,32]{2,1,0:T(1,128)S(1)} async-done(((f32[16,1,32]{2,1,0:T(1,128)}), f32[16,1,32]{2,1,0:T(1,128)S(1)}, u32[]{:S(2)}, u32[]{:S(2)}) %all-to-all-start.3) | async-done | bytes 2080 | tf_op jit(solution)/shard_map/all_to_all | solution.py:28
  435.8 0.5 add_sqrt_fusion
  (42 shorter events, 1.7 us)
Async XLA Ops:
  10.2 95.7 %copy-start.1 = (f32[1,2,4,4,2,256]{5,4,3,2,1,0:T(2,128)S(1)}, f32[1,2,4,4,2,256]{5,4,3,2,1,0:T(2,128)}, u32[]{:S(2)}) copy-start(f32[1,2,4,4,2,256]{5,4,3,2,1,0:T(2,128)} %param.9) | copy-start | bytes 196612
  108.2 6.7 %copy-start.2 = (s32[64]{0:T(128)S(1)}, s32[64]{0:T(128)}, u32[]{:S(2)}) copy-start(s32[64]{0:T(128)} %param.8) | copy-start | bytes 772
  108.2 105.7 %all-to-all-start = ((f32[32,1,2,4,4,2,256]{6,5,4,3,2,1,0:T(2,128)}), f32[32,1,2,4,4,2,256]{6,5,4,3,2,1,0:T(2,128)}, u32[]{:S(2)}, u32[]{:S(2)}) async-start(f32[32,1,2,4,4,2,256]{6,5,4,3,2,1,0:T(2,128)} %stack.40), calls=%async_computation | async-start | bytes 4194304 | tf_op jit(solution)/shard_map/all_to_all | solution.py:68
  114.7 183.1 %reduce-scatter.3.cloned.1.call-start = ((), (), s32[]{:S(2)}) async-start(), calls=%async_computation.6 | async-start | bytes 4718592 | tf_op jit(solution)/shard_map/reduce_scatter | solution.py:22
  272.3 1.6 copy-start.3
  281.6 138.9 %copy-start = (f32[32,1,2,384]{3,2,1,0:T(2,128)S(1)}, f32[32,1,2,384]{3,2,1,0:T(2,128)}, u32[]{:S(2)}) copy-start(f32[32,1,2,384]{3,2,1,0:T(2,128)} %param.11) | copy-start | bytes 294916
  281.7 138.9 %reduce-scatter.5.cloned.1.call-start = ((), (), s32[]{:S(2)}) async-start(), calls=%async_computation.7 | async-start | bytes 1671168 | tf_op jit(solution)/shard_map/reduce_scatter | solution.py:23
  422.2 13.6 %all-to-all-start.3 = ((f32[16,1,32]{2,1,0:T(1,128)}), f32[16,1,32]{2,1,0:T(1,128)S(1)}, u32[]{:S(2)}, u32[]{:S(2)}) async-start(f32[16,1,32]{2,1,0:T(1,128)} %broadcast_in_dim.12), calls=%async_computation.5 | async-start | bytes 16384 | tf_op jit(solution)/shard_map/all_to_all | solution.py:28
Sparse Core Ops, SparseCore 0:
  281.8 15.9 reduce-scatter.2
  301.9 118.6 reduce-scatter.4
